TPU v7x, 32 devices: a whole 2x2x4 slice. The times are simulated.
32 devices in a mesh: dp: 8 (over z, y), owner: 4 (over x, core).
Axes of the slice: x: 2, y: 2, z: 4, core: 2. Of those that a mesh axis runs over, the one named last changes fastest.
Arguments:
- grads: float32 [8, 32, 512, 128], P('dp', None, 'owner'), may hold values from -21 to 21
- momentum: float32 [64, 512, 128], P('dp', 'owner'), may hold values from -30 to 30
- slot_matrix: int32 [64], replicated, may hold values from -1 to 31, as said below
Outputs:
- updates: bfloat16 [32, 512, 128], P(None, 'owner')
- momentum_out: float32 [64, 512, 128], P('dp', 'owner')
Inputs may be any that keep to these rules, and one draw needn't show every extreme that they name: `slot_matrix`: entry s names the block held by slot s, or is -1 if slot s is empty; slots s with s // 8 == g belong to the owner group at index g of dp. Every one of the 32 blocks is held by exactly one slot, and some group, drawn from the seed, has all 8 slots filled.
All inputs are finite; a program needn't handle non-finite values.
Results may differ from a plain program's by a relative error of at most 0.038.
Values may be sent and summed in bfloat16 or wider, within the bound.
A program may use at most 64 MiB of HBM per device.

v0:
```python
import math
import jax
import jax.numpy as jnp
from jax import lax
from jax.sharding import PartitionSpec as P

C = 512
ITERS = 5
momentum_rate = 0.95
epsilon_norm = 1e-07
first_coef = 3.4445
third_coef = -4.775
fifth_coef = 2.0315


def local_gram(iterate):
    return jnp.einsum("kcr,kcq->krq", iterate, iterate, preferred_element_type=jnp.float32)


def make_poly(gram_matrix):
    square = jnp.einsum(
        "krq,kqp->krp", gram_matrix, gram_matrix, preferred_element_type=jnp.float32
    )
    return (third_coef * gram_matrix.astype(jnp.float32) + fifth_coef * square).astype(jnp.bfloat16)


def advance(iterate, polynomial):
    product = jnp.einsum("kcr,krq->kcq", iterate, polynomial, preferred_element_type=jnp.float32)
    return first_coef * iterate.astype(jnp.float32) + product


def whole_sweeps(iterate):
    for iteration in range(ITERS - 1):
        polynomial = make_poly(local_gram(iterate).astype(jnp.bfloat16))
        iterate = advance(iterate, polynomial).astype(jnp.bfloat16)
    return (iterate, make_poly(local_gram(iterate).astype(jnp.bfloat16)))


def finish(iterate, polynomial):
    return (math.sqrt(C) * advance(iterate, polynomial)).astype(jnp.bfloat16)


def local(grads, momentum, slot_matrix):
    partial_value = grads[0]
    present = (slot_matrix >= 0).astype(jnp.float32)
    picked = jnp.take(partial_value, jnp.maximum(slot_matrix, 0), axis=0) * present[:, None, None]
    summed = lax.psum_scatter(picked, "dp", scatter_dimension=0, tiled=True)
    renewed = momentum_rate * momentum + summed
    squares = lax.psum(jnp.sum(renewed * renewed, axis=(1, 2)), "owner")
    initial = (renewed / (jnp.sqrt(squares) + epsilon_norm)[:, None, None]).astype(jnp.bfloat16)
    iterate, polynomial = whole_sweeps(
        lax.all_to_all(initial, "owner", split_axis=0, concat_axis=1, tiled=True)
    )
    spread = finish(iterate, polynomial)
    update = lax.all_to_all(spread, "owner", split_axis=1, concat_axis=0, tiled=True)
    everyone = lax.all_gather(update, "dp", axis=0, tiled=True)
    all_slots = everyone.shape[0]
    matches = slot_matrix[None, :] == jnp.arange(grads.shape[1], dtype=jnp.int32)[:, None]
    slot_of = jnp.sum(
        jnp.where(matches, jnp.arange(all_slots, dtype=jnp.int32)[None, :], 0), axis=1
    )
    return (jnp.take(everyone, slot_of, axis=0), renewed)


def solution(mesh):
    return jax.shard_map(
        local,
        mesh=mesh,
        in_specs=(P("dp", None, "owner", None), P("dp", "owner", None), P()),
        out_specs=(P(None, "owner", None), P("dp", "owner", None)),
        check_vma=False,
    )
```

profile of v0, /device:TPU:0, one launch (start us, length us, event | category | flops | bytes accessed | tf_op | source)
XLA Modules:
  0.0 194.9 jit_solution(15638819623874804117)
XLA Ops:
  7.2 0.0 copy-start
  7.2 0.0 reduce-scatter.2.cloned.1.call-start
  7.2 0.8 broadcast_compare_fusion
  8.0 0.7 broadcast_maximum_fusion
  8.7 0.1 copy-done
  8.8 2.8 %gather_fusion = f32[64,128,128]{2,1,0:T(8,128)} fusion(f32[32,128,128]{2,1,0:T(8,128)S(1)} %bitcast.38, s32[1024]{0:T(1024)S(1)} %pad_clamp_fusion.1), kind=kCustom, calls=%fused_computation | custom fusion | bytes 8388864 | tf_op jit(solution)/shard_map/jit(_take)/gather | solution.py:46
  11.5 4.6 %select_multiply_fusion = f32[64,128,128]{2,1,0:T(8,128)} fusion(f32[64,128,128]{2,1,0:T(8,128)} %gather_fusion, f32[64]{0:T(128)S(1)} %get-tuple-element.5, pred[64]{0:T(512)(128)(4,1)S(1)} %get-tuple-element.4), kind=kLoop, calls=%fused_computation.2 | loop fusion | flops 2097152 | bytes 8388928 | tf_op jit(solution)/shard_map/mul | solution.py:46
  16.1 0.0 copy-start.2
  16.1 0.0 reduce-scatter.2.cloned.1.call-update
  16.1 0.0 all-gather.2.cloned.1.call-start
  16.2 91.1 %reduce-scatter.2.cloned.1.call-done = f32[8,128,128]{2,1,0:T(8,128)} async-done(((f32[64,128,128]{2,1,0:T(8,128)}), f32[8,128,128]{2,1,0:T(8,128)}) %reduce-scatter.2.cloned.1.call-update) | async-done | bytes 524304 | tf_op jit(solution)/shard_map/reduce_scatter | solution.py:47
  107.3 0.0 copy-done.2
  107.3 1.2 multiply_reduce_fusion
  108.5 0.0 copy-start.1
  108.5 6.2 %psum.7 = f32[8]{0:T(128)S(1)} all-reduce(f32[8]{0:T(128)S(1)} %get-tuple-element.2), channel_id=1, replica_groups=mesh['dp'=8,'owner'=4] {'owner'}, use_global_device_ids=true, to_apply=%region_3.4 | all-reduce | flops 8 | bytes 64 | tf_op jit(solution)/shard_map/psum | solution.py:49
  114.7 0.1 divide_convert_fusion
  114.8 8.4 %all_to_all.36 = bf16[8,128,128]{2,1,0:T(8,128)(2,1)S(1)} all-to-all(bf16[8,128,128]{2,1,0:T(8,128)(2,1)S(1)} %divide_convert_fusion), channel_id=1, replica_groups=mesh['dp'=8,'owner'=4] {'owner'}, dimensions={0} | all-to-all | bytes 524288 | tf_op jit(solution)/shard_map/all_to_all | solution.py:52
  123.2 0.0 copy-done.1
  123.3 0.3 convolution_convert_fusion.4
  123.5 0.0 copy-start.3
  123.5 0.4 fusion.2
  123.9 0.3 convolution_convert_fusion.3
  124.2 0.4 fusion.3
  124.6 0.3 convolution_convert_fusion.2
  124.8 0.4 fusion.4
  125.2 0.3 convolution_convert_fusion.1
  125.5 0.4 fusion.5
  125.9 0.3 convolution_convert_fusion
  126.1 0.4 fusion.1
  126.5 0.3 copy.40
  126.8 8.4 %all_to_all.37 = bf16[2,512,128]{2,0,1:T(2,128)(2,1)S(1)} all-to-all(bf16[2,512,128]{2,0,1:T(2,128)(2,1)S(1)} %copy.40), channel_id=1, replica_groups=mesh['dp'=8,'owner'=4] {'owner'}, dimensions={1} | all-to-all | bytes 524288 | tf_op jit(solution)/shard_map/all_to_all | solution.py:55
  135.2 0.7 copy.42
  135.9 0.0 all-gather.2.cloned.1.call-update
  136.0 0.0 copy-done.3
  136.0 0.1 select_reduce_fusion
  136.1 48.5 %all-gather.2.cloned.1.call-done = bf16[64,128,128]{2,1,0:T(8,128)(2,1)} async-done(((bf16[8,128,128]{2,1,0:T(8,128)(2,1)}), bf16[64,128,128]{2,1,0:T(8,128)(2,1)}) %all-gather.2.cloned.1.call-update) | async-done | bytes 2097168 | tf_op jit(solution)/shard_map/all_gather | solution.py:56
  184.6 2.3 %gather_fusion.1 = bf16[32,128,128]{2,1,0:T(8,128)(2,1)S(1)} fusion(bf16[64,128,128]{2,1,0:T(8,128)(2,1)} %all-gather.2.cloned.1.call-done, s32[1024]{0:T(1024)S(1)} %pad_clamp_fusion), kind=kCustom, calls=%fused_computation.1 | custom fusion | bytes 2097280 | tf_op jit(solution)/shard_map/jit(_take)/gather | solution.py:62
  186.9 1.1 broadcast_select_fusion
  (7 shorter events, 0.1 us)
Async XLA Ops:
  7.2 1.6 copy-start
  7.2 100.1 %reduce-scatter.2.cloned.1.call-start = ((), (), s32[]{:S(2)}) async-start(), calls=%async_computation.3 | async-start | bytes 4718592 | tf_op jit(solution)/shard_map/reduce_scatter | solution.py:47
  16.1 91.2 %copy-start.2 = (f32[8,128,128]{2,1,0:T(8,128)S(1)}, f32[8,128,128]{2,1,0:T(8,128)}, u32[]{:S(2)}) copy-start(f32[8,128,128]{2,1,0:T(8,128)} %param.4) | copy-start | bytes 1572868
  16.1 168.5 %all-gather.2.cloned.1.call-start = ((), (), s32[]{:S(2)}) async-start(), calls=%async_computation.4 | async-start | bytes 2359296 | tf_op jit(solution)/shard_map/all_gather | solution.py:56
  108.5 14.7 %copy-start.1 = (f32[8,128,128]{2,1,0:T(8,128)}, f32[8,128,128]{2,1,0:T(8,128)S(1)}, u32[]{:S(2)}) copy-start(f32[8,128,128]{2,1,0:T(8,128)S(1)} %get-tuple-element.3) | copy-start | bytes 1572868
  123.5 12.4 %copy-start.3 = (s32[64]{0:T(128)S(1)}, s32[64]{0:T(128)}, u32[]{:S(2)}) copy-start(s32[64]{0:T(128)} %param.5) | copy-start | bytes 772
Sparse Core Ops, SparseCore 0:
  16.2 91.0 reduce-scatter.1
  136.1 48.4 all-gather.1
where the time goes:
time: 195 us
  waiting for transfers between devices  140 us (72%)
  blocking collectives  23 us (12%)
  between operations  14.2 us (7%)
  other arithmetic  8.63 us (4%)
  local copies, waits for them, and re-layouts  6.24 us (3%)
  matrix products  3.19 us (2%)
    reduce_scatter x1, waiting for transfers between devices, local(): summed = lax.psum_scatter(picked, 'dp', scatter_dimension=0, tiled=True)  91.1 us
    all_gather x1, waiting for transfers between devices, local(): everyone = lax.all_gather(update, 'dp', axis=0, tiled=True)  48.5 us
    all_to_all x1, blocking collectives, local(): lax.all_to_all(initial, 'owner', split_axis=0, concat_axis=1, tiled=True)  8.39 us
    all_to_all x1, blocking collectives, local(): lax.all_to_all(spread, 'owner', split_axis=1, concat_axis=0, tiled=True)  8.39 us
    psum x1, blocking collectives, local(): squares = lax.psum(jnp.sum(renewed * renewed, axis=(1, 2)), 'owner')  6.2 us
    mul x1, other arithmetic, local(): jnp.take(partial_value, jnp.maximum(slot_matrix, 0), axis=0)  4.55 us
  transfers between devices with their start and end apart: 2, of which 2 were waited for; matrix products, arithmetic and copies ran while one was open for 0% of the time, Pallas kernels for 0%

commit v1 on v0

--- a/solution.py
+++ b/solution.py
@@ -53,7 +53,14 @@
     )
     spread = finish(iterate, polynomial)
     update = lax.all_to_all(spread, "owner", split_axis=1, concat_axis=0, tiled=True)
-    everyone = lax.all_gather(update, "dp", axis=0, tiled=True)
+    size = lax.axis_size("dp")
+    hops = [(i, (i + 1) % size) for i in range(size)]
+    terms = [update]
+    for far in range(1, size):
+        terms = [lax.ppermute(terms[0], "dp", hops), *terms]
+    result = jnp.concatenate(terms, axis=0)
+    shift = (lax.axis_index("dp") + 1) * terms[-1].shape[0]
+    everyone = jnp.roll(result, shift, axis=0)
     all_slots = everyone.shape[0]
     matches = slot_matrix[None, :] == jnp.arange(grads.shape[1], dtype=jnp.int32)[:, None]
     slot_of = jnp.sum(

time: 195 us -> 221 us (1.13)
  waiting for transfers between devices: 140 us -> 157 us
  local copies, waits for them, and re-layouts: 6.24 us -> 13 us
    ppermute x0 -> x7, waiting for transfers between devices: none -> 65.4 us  [local(): terms = [lax.ppermute(terms[0], 'dp', hops), *terms]]
    all_gather x1 -> x0, waiting for transfers between devices: 48.5 us -> none  [local(): everyone = lax.all_gather(update, 'dp', axis=0, tiled=True)]
    unnamed x8 -> x25, local copies, waits for them, and re-layouts: 0.1 us -> 6 us
  transfers between devices with their start and end apart: 2 -> 8, of which waited for: 2 -> 8; matrix products, arithmetic and copies ran while one was open for 0% -> 0% of each run, Pallas kernels for 0% -> 0%
where the time goes in v1:
time: 221 us
  waiting for transfers between devices  157 us (71%)
  blocking collectives  23 us (10%)
  between operations  14.3 us (6%)
  local copies, waits for them, and re-layouts  13 us (6%)
  other arithmetic  9.29 us (4%)
  matrix products  3.2 us (1%)
    reduce_scatter x1, waiting for transfers between devices, local(): summed = lax.psum_scatter(picked, 'dp', scatter_dimension=0, tiled=True)  91.2 us
    ppermute x7, waiting for transfers between devices, local(): terms = [lax.ppermute(terms[0], 'dp', hops), *terms]  65.4 us
    all_to_all x1, blocking collectives, local(): lax.all_to_all(initial, 'owner', split_axis=0, concat_axis=1, tiled=True)  8.39 us
    all_to_all x1, blocking collectives, local(): lax.all_to_all(spread, 'owner', split_axis=1, concat_axis=0, tiled=True)  8.39 us
    psum x1, blocking collectives, local(): squares = lax.psum(jnp.sum(renewed * renewed, axis=(1, 2)), 'owner')  6.2 us
    unnamed x25, local copies, waits for them, and re-layouts  6 us
    mul x1, other arithmetic, local(): jnp.take(partial_value, jnp.maximum(slot_matrix, 0), axis=0)  4.56 us
  transfers between devices with their start and end apart: 8, of which 8 were waited for; matrix products, arithmetic and copies ran while one was open for 0% of the time, Pallas kernels for 0%

profile of v1, /device:TPU:0, one launch (start us, length us, event | category | flops | bytes accessed | tf_op | source)
XLA Modules:
  0.0 220.9 jit_solution(4572982670919440507)
XLA Ops:
  7.2 0.0 copy-start
  7.2 0.0 reduce-scatter.2.cloned.1.call-start
  7.2 0.9 select_reduce_fusion
  8.1 0.7 broadcast_maximum_fusion
  8.8 0.7 broadcast_compare_fusion
  9.5 0.0 copy-done
  9.5 2.8 %gather_fusion = f32[64,128,128]{2,1,0:T(8,128)} fusion(f32[32,128,128]{2,1,0:T(8,128)S(1)} %bitcast.38, s32[1024]{0:T(1024)S(1)} %get-tuple-element.7), kind=kCustom, calls=%fused_computation | custom fusion | bytes 8388864 | tf_op jit(solution)/shard_map/jit(_take)/gather | solution.py:46
  12.2 4.6 %select_multiply_fusion = f32[64,128,128]{2,1,0:T(8,128)} fusion(f32[64,128,128]{2,1,0:T(8,128)} %gather_fusion, f32[64]{0:T(128)S(1)} %get-tuple-element.5, pred[64]{0:T(512)(128)(4,1)S(1)} %get-tuple-element.4), kind=kLoop, calls=%fused_computation.2 | loop fusion | flops 2097152 | bytes 8388928 | tf_op jit(solution)/shard_map/mul | solution.py:46
  16.8 0.0 copy-start.4
  16.8 0.0 reduce-scatter.2.cloned.1.call-update
  16.8 91.2 %reduce-scatter.2.cloned.1.call-done = f32[8,128,128]{2,1,0:T(8,128)} async-done(((f32[64,128,128]{2,1,0:T(8,128)}), f32[8,128,128]{2,1,0:T(8,128)}) %reduce-scatter.2.cloned.1.call-update) | async-done | bytes 524304 | tf_op jit(solution)/shard_map/reduce_scatter | solution.py:47
  108.0 0.0 copy-done.4
  108.0 1.2 multiply_reduce_fusion
  109.2 0.0 copy-start.1
  109.2 6.2 %psum.7 = f32[8]{0:T(128)S(1)} all-reduce(f32[8]{0:T(128)S(1)} %get-tuple-element.2), channel_id=1, replica_groups=mesh['dp'=8,'owner'=4] {'owner'}, use_global_device_ids=true, to_apply=%region_3.4 | all-reduce | flops 8 | bytes 64 | tf_op jit(solution)/shard_map/psum | solution.py:49
  115.4 0.1 divide_convert_fusion
  115.6 8.4 %all_to_all.36 = bf16[8,128,128]{2,1,0:T(8,128)(2,1)S(1)} all-to-all(bf16[8,128,128]{2,1,0:T(8,128)(2,1)S(1)} %divide_convert_fusion), channel_id=1, replica_groups=mesh['dp'=8,'owner'=4] {'owner'}, dimensions={0} | all-to-all | bytes 524288 | tf_op jit(solution)/shard_map/all_to_all | solution.py:52
  124.0 0.0 copy-done.1
  124.0 0.3 convolution_convert_fusion.4
  124.3 0.4 fusion.2
  124.6 0.3 convolution_convert_fusion.3
  124.9 0.4 fusion.3
  125.3 0.3 convolution_convert_fusion.2
  125.5 0.4 fusion.4
  125.9 0.3 convolution_convert_fusion.1
  126.2 0.4 fusion.5
  126.6 0.3 convolution_convert_fusion
  126.8 0.4 fusion.1
  127.2 0.3 copy.40
  127.5 8.4 %all_to_all.37 = bf16[2,512,128]{2,0,1:T(2,128)(2,1)S(1)} all-to-all(bf16[2,512,128]{2,0,1:T(2,128)(2,1)S(1)} %copy.40), channel_id=1, replica_groups=mesh['dp'=8,'owner'=4] {'owner'}, dimensions={1} | all-to-all | bytes 524288 | tf_op jit(solution)/shard_map/all_to_all | solution.py:55
  136.0 1.5 collective-permute-start
  137.5 8.9 %collective-permute-done = bf16[8,128,128]{2,1,0:T(8,128)(2,1)S(1)} collective-permute-done((bf16[8,128,128]{2,1,0:T(8,128)(2,1)S(1)}, bf16[8,128,128]{2,1,0:T(8,128)(2,1)S(1)}, u32[]{:S(2)}, u32[]{:S(2)}) %collective-permute-start) | collective-permute-done | bytes 262176 | tf_op jit(solution)/shard_map/ppermute | solution.py:60
  146.4 0.0 collective-permute-start.1
  146.4 9.5 %collective-permute-done.1 = bf16[8,128,128]{2,1,0:T(8,128)(2,1)S(1)} collective-permute-done((bf16[8,128,128]{2,1,0:T(8,128)(2,1)S(1)}, bf16[8,128,128]{2,1,0:T(8,128)(2,1)S(1)}, u32[]{:S(2)}, u32[]{:S(2)}) %collective-permute-start.1) | collective-permute-done | bytes 262176 | tf_op jit(solution)/shard_map/ppermute | solution.py:60
  155.9 0.0 collective-permute-start.2
  155.9 9.1 %collective-permute-done.2 = bf16[8,128,128]{2,1,0:T(8,128)(2,1)S(1)} collective-permute-done((bf16[8,128,128]{2,1,0:T(8,128)(2,1)S(1)}, bf16[8,128,128]{2,1,0:T(8,128)(2,1)S(1)}, u32[]{:S(2)}, u32[]{:S(2)}) %collective-permute-start.2) | collective-permute-done | bytes 262176 | tf_op jit(solution)/shard_map/ppermute | solution.py:60
  165.0 0.0 collective-permute-start.3
  165.0 9.1 %collective-permute-done.3 = bf16[8,128,128]{2,1,0:T(8,128)(2,1)S(1)} collective-permute-done((bf16[8,128,128]{2,1,0:T(8,128)(2,1)S(1)}, bf16[8,128,128]{2,1,0:T(8,128)(2,1)S(1)}, u32[]{:S(2)}, u32[]{:S(2)}) %collective-permute-start.3) | collective-permute-done | bytes 262176 | tf_op jit(solution)/shard_map/ppermute | solution.py:60
  174.0 0.0 collective-permute-start.4
  174.0 9.1 %collective-permute-done.4 = bf16[8,128,128]{2,1,0:T(8,128)(2,1)S(1)} collective-permute-done((bf16[8,128,128]{2,1,0:T(8,128)(2,1)S(1)}, bf16[8,128,128]{2,1,0:T(8,128)(2,1)S(1)}, u32[]{:S(2)}, u32[]{:S(2)}) %collective-permute-start.4) | collective-permute-done | bytes 262176 | tf_op jit(solution)/shard_map/ppermute | solution.py:60
  183.1 0.0 copy-start.2
  183.1 0.7 copy-done.2
  183.8 0.0 collective-permute-start.5
  183.8 10.4 %collective-permute-done.5 = bf16[8,128,128]{2,1,0:T(8,128)(2,1)} collective-permute-done((bf16[8,128,128]{2,1,0:T(8,128)(2,1)S(1)}, bf16[8,128,128]{2,1,0:T(8,128)(2,1)}, u32[]{:S(2)}, u32[]{:S(2)}) %collective-permute-start.5) | collective-permute-done | bytes 262176 | tf_op jit(solution)/shard_map/ppermute | solution.py:60
  194.2 0.0 collective-permute-start.6
  194.2 0.0 copy-start.3
  194.2 9.4 %collective-permute-done.6 = bf16[8,128,128]{2,1,0:T(8,128)(2,1)} collective-permute-done((bf16[8,128,128]{2,1,0:T(8,128)(2,1)}, bf16[8,128,128]{2,1,0:T(8,128)(2,1)}, u32[]{:S(2)}, u32[]{:S(2)}) %collective-permute-start.6) | collective-permute-done | bytes 262176 | tf_op jit(solution)/shard_map/ppermute | solution.py:60
  203.6 1.0 constant_dynamic-update-slice_fusion.15
  204.6 1.0 constant_dynamic-update-slice_fusion.14
  205.6 1.0 constant_dynamic-update-slice_fusion.13
  206.8 1.0 constant_dynamic-update-slice_fusion.7
  207.8 1.0 constant_dynamic-update-slice_fusion.6
  208.8 0.0 copy-done.3
  209.0 1.5 constant_dynamic-slice_fusion
  210.5 2.3 %gather_fusion.1 = bf16[32,128,128]{2,1,0:T(8,128)(2,1)S(1)} fusion(bf16[64,128,128]{2,1,0:T(8,128)(2,1)} %constant_dynamic-slice_fusion, s32[1024]{0:T(1024)S(1)} %get-tuple-element.6), kind=kCustom, calls=%fused_computation.1 | custom fusion | bytes 2097280 | tf_op jit(solution)/shard_map/jit(_take)/gather | solution.py:69
  212.9 1.1 broadcast_select_fusion
  (18 shorter events, 0.5 us)
Async XLA Ops:
  7.2 2.3 %copy-start = (f32[1,32,128,128]{3,2,1,0:T(8,128)S(1)}, f32[1,32,128,128]{3,2,1,0:T(8,128)}, u32[]{:S(2)}) copy-start(f32[1,32,128,128]{3,2,1,0:T(8,128)} %param.3) | copy-start | bytes 6291460
  7.2 100.8 %reduce-scatter.2.cloned.1.call-start = ((), (), s32[]{:S(2)}) async-start(), calls=%async_computation.3 | async-start | bytes 4718592 | tf_op jit(solution)/shard_map/reduce_scatter | solution.py:47
  16.8 91.2 %copy-start.4 = (f32[8,128,128]{2,1,0:T(8,128)S(1)}, f32[8,128,128]{2,1,0:T(8,128)}, u32[]{:S(2)}) copy-start(f32[8,128,128]{2,1,0:T(8,128)} %param.4) | copy-start | bytes 1572868
  109.2 14.7 %copy-start.1 = (f32[8,128,128]{2,1,0:T(8,128)}, f32[8,128,128]{2,1,0:T(8,128)S(1)}, u32[]{:S(2)}) copy-start(f32[8,128,128]{2,1,0:T(8,128)S(1)} %get-tuple-element.3) | copy-start | bytes 1572868
  136.0 10.4 %collective-permute-start = (bf16[8,128,128]{2,1,0:T(8,128)(2,1)S(1)}, bf16[8,128,128]{2,1,0:T(8,128)(2,1)S(1)}, u32[]{:S(2)}, u32[]{:S(2)}) collective-permute-start(bf16[8,128,128]{2,1,0:T(8,128)(2,1)S(1)} %bitcast.41), channel_id=1, source_target_pairs={{0,4},{4,8},{8,12},{12,16},{16,20},{20,24},{24,28},{28,0},{1,5},{5... | collective-permute-start | bytes 786440 | tf_op jit(solution)/shard_map/ppermute | solution.py:60
  146.4 9.5 %collective-permute-start.1 = (bf16[8,128,128]{2,1,0:T(8,128)(2,1)S(1)}, bf16[8,128,128]{2,1,0:T(8,128)(2,1)S(1)}, u32[]{:S(2)}, u32[]{:S(2)}) collective-permute-start(bf16[8,128,128]{2,1,0:T(8,128)(2,1)S(1)} %collective-permute-done), channel_id=1, source_target_pairs={{0,4},{4,8},{8,12},{12,16},{16,20},{20,24},{24,28},{28,0},{1,5},{5... | collective-permute-start | bytes 786440 | tf_op jit(solution)/shard_map/ppermute | solution.py:60
  155.9 9.1 %collective-permute-start.2 = (bf16[8,128,128]{2,1,0:T(8,128)(2,1)S(1)}, bf16[8,128,128]{2,1,0:T(8,128)(2,1)S(1)}, u32[]{:S(2)}, u32[]{:S(2)}) collective-permute-start(bf16[8,128,128]{2,1,0:T(8,128)(2,1)S(1)} %collective-permute-done.1), channel_id=1, source_target_pairs={{0,4},{4,8},{8,12},{12,16},{16,20},{20,24},{24,28},{28,0},{1,5},{5... | collective-permute-start | bytes 786440 | tf_op jit(solution)/shard_map/ppermute | solution.py:60
  165.0 9.1 %collective-permute-start.3 = (bf16[8,128,128]{2,1,0:T(8,128)(2,1)S(1)}, bf16[8,128,128]{2,1,0:T(8,128)(2,1)S(1)}, u32[]{:S(2)}, u32[]{:S(2)}) collective-permute-start(bf16[8,128,128]{2,1,0:T(8,128)(2,1)S(1)} %collective-permute-done.2), channel_id=1, source_target_pairs={{0,4},{4,8},{8,12},{12,16},{16,20},{20,24},{24,28},{28,0},{1,5},{5... | collective-permute-start | bytes 786440 | tf_op jit(solution)/shard_map/ppermute | solution.py:60
  174.0 9.1 %collective-permute-start.4 = (bf16[8,128,128]{2,1,0:T(8,128)(2,1)S(1)}, bf16[8,128,128]{2,1,0:T(8,128)(2,1)S(1)}, u32[]{:S(2)}, u32[]{:S(2)}) collective-permute-start(bf16[8,128,128]{2,1,0:T(8,128)(2,1)S(1)} %collective-permute-done.3), channel_id=1, source_target_pairs={{0,4},{4,8},{8,12},{12,16},{16,20},{20,24},{24,28},{28,0},{1,5},{5... | collective-permute-start | bytes 786440 | tf_op jit(solution)/shard_map/ppermute | solution.py:60
  183.1 0.7 copy-start.2
  183.8 10.4 %collective-permute-start.5 = (bf16[8,128,128]{2,1,0:T(8,128)(2,1)S(1)}, bf16[8,128,128]{2,1,0:T(8,128)(2,1)}, u32[]{:S(2)}, u32[]{:S(2)}) collective-permute-start(bf16[8,128,128]{2,1,0:T(8,128)(2,1)S(1)} %collective-permute-done.4), channel_id=1, source_target_pairs={{0,4},{4,8},{8,12},{12,16},{16,20},{20,24},{24,28},{28,0},{1,5},{5... | collective-permute-start | bytes 786440 | tf_op jit(solution)/shard_map/ppermute | solution.py:60
  194.2 9.4 %collective-permute-start.6 = (bf16[8,128,128]{2,1,0:T(8,128)(2,1)}, bf16[8,128,128]{2,1,0:T(8,128)(2,1)}, u32[]{:S(2)}, u32[]{:S(2)}) collective-permute-start(bf16[8,128,128]{2,1,0:T(8,128)(2,1)} %collective-permute-done.5), channel_id=1, source_target_pairs={{0,4},{4,8},{8,12},{12,16},{16,20},{20,24},{24,28},{28,0},{1,5},{5... | collective-permute-start | bytes 786440 | tf_op jit(solution)/shard_map/ppermute | solution.py:60
  194.2 14.5 %copy-start.3 = (bf16[8,128,128]{2,1,0:T(8,128)(2,1)S(1)}, bf16[8,128,128]{2,1,0:T(8,128)(2,1)}, u32[]{:S(2)}) copy-start(bf16[8,128,128]{2,1,0:T(8,128)(2,1)} %copy-done.2) | copy-start | bytes 786436
Sparse Core Ops, SparseCore 0:
  16.9 91.0 reduce-scatter.1
